TPU v7x, 32 devices: a whole 2x2x4 slice. The times are simulated.
32 devices in a mesh: env: 4 (over z), cand: 8 (over y, x, core).
Axes of the slice: x: 2, y: 2, z: 4, core: 2. Of those that a mesh axis runs over, the one named last changes fastest.
Arguments:
- white: bfloat16 [3, 64, 64, 4096], P(None, 'env', 'cand'), may hold values from -5 to 5
- mean_init: float32 [64, 2560], P('env'), may hold values from -0.3 to 0.3
- std_init: float32 [64, 2560], P('env'), may hold values from 0.05 to 0.8
- init_state: float32 [64, 128], P('env'), may hold values from -3 to 3
- goal_state: float32 [64, 128], P('env'), may hold values from -3 to 3
- w_state: bfloat16 [128, 512], replicated, may hold values from -0.5 to 0.5
- w_action: bfloat16 [64, 512], replicated, may hold values from -1.5 to 1.5
- w_out: bfloat16 [512, 128], replicated, may hold values from -0.25 to 0.25
- bias_in: float32 [512], replicated, may hold values from -3 to 3
- bias_out: float32 [128], replicated, may hold values from -3 to 3
- elite_idx: int32 [64, 3, 6], P('env'), may hold values from 0 to 63, all different within a row
Outputs:
- final_mean: float32 [64, 2560], P('env')
- final_std: float32 [64, 2560], P('env')
- costs: float32 [3, 64, 64], P(None, 'env', 'cand')
Inputs may be any that keep to these rules, and one draw needn't show every extreme that they name: `elite_idx`: each row names 6 different candidates.
All inputs are finite; a program needn't handle non-finite values.
Results may differ from a plain program's by a relative error of at most 0.0031.
Values sent between devices are 32-bit elements; how exact they have to be, the bound alone decides.
A program may use at most 128 MiB of HBM per device.

v0:
```python
import functools

import jax
import jax.numpy as jnp
import numpy as np
from jax import lax
from jax.experimental import pallas as pl
from jax.experimental.pallas import tpu as pltpu
from jax.sharding import PartitionSpec as P

BETA_EXP = 2.5
MOMENTUM = 0.1
FLOOR_SHARE = 0.1
ACT_COST = 0.1
MESH = pl.DeviceIdType.MESH
LANES = 128
WIDE = 256
SUB = 8

WHILE_SUMS = ((), ((0, 12, 20), (1, 0, 10)), ((2, 0, 14),))
WHILE_PEAKS = (((0, 0, 6),), ((1, 10, 15),), ((2, 14, 20),))
WHILE_MOMENTS = (((0, 6, 12),), ((1, 15, 20),), ())


def color_rows(length, act):
    freqs = np.arange(length // 2 + 1)
    scale = (np.maximum(freqs, 1) / length) ** (-BETA_EXP / 2)
    kernel = np.fft.irfft(scale, n=length)
    kernel = kernel / np.sqrt(np.sum(kernel * kernel))
    q = WIDE // act
    row = np.arange(length)
    lane_step = np.arange(WIDE) // act
    shift = (q * (row // q))[:, None] + lane_step[None, :] - (row % q)[:, None]
    return jnp.asarray(kernel[shift % length], dtype=jnp.bfloat16).astype(jnp.float32)


def plan_kernel(
    dims,
    white_hbm,
    mean_ref,
    std_ref,
    start_ref,
    goal_ref,
    ws_ref,
    wa_ref,
    wo_ref,
    bi_ref,
    bo_ref,
    elite_ref,
    color_ref,
    fmean_ref,
    fstd_ref,
    cost_out,
    white,
    table,
    noise,
    acts,
    w_pair,
    state,
    goals,
    cost,
    member,
    cen,
    spr,
    part,
    rs_recv,
    ag,
    z_send,
    z_recv,
    p_send,
    p_recv,
    copy_sem,
    send_sem,
    recv_sem,
):
    iters, env_dev, cand_dev, act, tiles, units, share, n_cand, n_env, elites = dims
    rows = env_dev * cand_dev
    state_dim = start_ref.shape[1]
    halves = env_dev // SUB
    n_units = tiles * halves
    length_blocks = white.shape[1] // WIDE
    out_blocks = tiles * LANES // WIDE
    low_block = length_blocks - out_blocks + 1
    per_tile = LANES // act
    me = lax.axis_index("cand")
    me_env = lax.axis_index("env")

    loads = []
    for at, first, size in ((0, 0, rows), (1, rows, (iters - 1) * rows)):
        spot = pl.ds(first, size)
        loads.append(pltpu.make_async_copy(white_hbm.at[spot], white.at[spot], copy_sem.at[at]))
        loads[at].start()

    barrier = pltpu.get_barrier_semaphore()
    for o in range(1, n_cand):
        pl.semaphore_signal(
            barrier, inc=1, device_id={"cand": lax.rem(me + o, n_cand)}, device_id_type=MESH
        )
    for o in range(1, n_env):
        pl.semaphore_signal(
            barrier, inc=1, device_id={"env": lax.rem(me_env + o, n_env)}, device_id_type=MESH
        )

    q = WIDE // act
    eye = (
        lax.broadcasted_iota(jnp.int32, (act, WIDE), 0)
        == lax.broadcasted_iota(jnp.int32, (act, WIDE), 1) % act
    )

    def build(block, carry):
        shift = lax.rem(2 * length_blocks - (block + low_block), length_blocks)
        for j in range(q):
            line = color_ref[shift, j : j + 1, :]
            piece = jnp.where(eye, line, 0.0).astype(jnp.bfloat16)
            table[pl.ds(pl.multiple_of(block * WIDE + j * act, act), act), :] = piece
        return carry

    lax.fori_loop(0, table.shape[0] // WIDE, build, 0)

    w_pair[...] = jnp.zeros_like(w_pair)
    for p in range(per_tile):
        w_pair[p, :state_dim, :] = ws_ref[...] * jnp.bfloat16(0.5)
        w_pair[p, state_dim + p * act : state_dim + (p + 1) * act, :] = wa_ref[...] * jnp.bfloat16(0.5)
    for it in range(iters):
        own = elite_ref[it]
        for c in range(cand_dev):
            hit = (own == me * cand_dev + c).astype(jnp.float32)
            hit = jnp.sum(hit, axis=1, keepdims=True)
            member[it, c] = jnp.broadcast_to(hit, (env_dev, LANES))
    for c in range(cand_dev):
        spot = slice(c * env_dev, (c + 1) * env_dev)
        goals[spot, :] = goal_ref[...]
        for it in range(iters):
            state[it, spot, :] = start_ref[...]
    cost[...] = jnp.zeros_like(cost)
    if units > n_units:
        cen[...] = jnp.zeros_like(cen)
        spr[...] = jnp.zeros_like(spr)
        part[...] = jnp.zeros_like(part)
    for tile in range(tiles):
        for h in range(halves):
            at = (slice(h * SUB, (h + 1) * SUB), slice(tile * LANES, (tile + 1) * LANES))
            cen[tile * halves + h] = mean_ref[at]
            spr[tile * halves + h] = std_ref[at]

    def color(first, size):
        spot = slice(first, first + size)

        def one(block, carry):
            start = pl.multiple_of((out_blocks - 1 - block) * WIDE, WIDE)
            band = table[pl.ds(start, white.shape[1]), :]
            out = jnp.dot(white[spot, :], band, preferred_element_type=jnp.float32)
            for p in range(WIDE // LANES):
                noise[block * (WIDE // LANES) + p, spot, :] = out[:, p * LANES : (p + 1) * LANES]
            return carry

        lax.fori_loop(0, out_blocks, one, 0)

    act_weight = ACT_COST * state_dim / act

    def make_actions(it):
        def one(tile, carry):
            unit = pl.ds(tile * halves, halves)
            center = cen[unit].reshape(env_dev, LANES)
            spread = spr[unit].reshape(env_dev, LANES)
            sums = jnp.zeros((env_dev, LANES), jnp.float32)
            squares = jnp.zeros((env_dev, LANES), jnp.float32)
            for c in range(cand_dev):
                drawn = noise[tile, pl.ds(it * rows + c, env_dev, stride=cand_dev), :]
                action = jnp.clip(center + spread * drawn, -1.0, 1.0)
                spot = slice(c * env_dev, (c + 1) * env_dev)
                acts[it, tile, spot, :] = action.astype(jnp.bfloat16)
                chosen = member[it, c] * action
                square = action * action
                sums = sums + chosen
                squares = squares + chosen * action
                cost[it, spot, :] += act_weight * square
            sums = sums.reshape(halves, SUB, LANES)
            squares = squares.reshape(halves, SUB, LANES)
            for h in range(halves):
                part[it, tile * halves + h, 0] = sums[h]
                part[it, tile * halves + h, 1] = squares[h]
            return carry

        lax.fori_loop(0, tiles, one, 0)

    def scatter_copies(it):
        for o in range(1, n_cand):
            peer = lax.rem(me + o, n_cand)
            yield pltpu.make_async_remote_copy(
                src_ref=part.at[it, pl.ds(peer * share, share)],
                dst_ref=rs_recv.at[it, o - 1],
                send_sem=send_sem.at[it, 0],
                recv_sem=recv_sem.at[it, 0],
                device_id={"cand": peer},
                device_id_type=MESH,
            )

    def gather_copies(it):
        mine = ag.at[it, pl.ds(me * share, share)]
        for o in range(1, n_cand):
            yield pltpu.make_async_remote_copy(
                src_ref=mine,
                dst_ref=mine,
                send_sem=send_sem.at[it, 1],
                recv_sem=recv_sem.at[it, 1],
                device_id={"cand": lax.rem(me + o, n_cand)},
                device_id_type=MESH,
            )

    def row_copies(it):
        for o in range(1, n_cand):
            yield pltpu.make_async_remote_copy(
                src_ref=p_send.at[it],
                dst_ref=p_recv.at[it, o - 1],
                send_sem=send_sem.at[it, 3],
                recv_sem=recv_sem.at[it, 3],
                device_id={"cand": lax.rem(me + o, n_cand)},
                device_id_type=MESH,
            )

    def peak_copies(it):
        for o in range(1, n_env):
            yield pltpu.make_async_remote_copy(
                src_ref=z_send.at[it],
                dst_ref=z_recv.at[it, o - 1],
                send_sem=send_sem.at[it, 2],
                recv_sem=recv_sem.at[it, 2],
                device_id={"env": lax.rem(me_env + o, n_env)},
                device_id_type=MESH,
            )

    def await_bytes(stage, it, sem):
        others = (n_cand - 1) * share
        ref = (rs_recv.at[it], ag.at[it, pl.ds(0, others)], z_recv.at[it], p_recv.at[it])[stage]
        pltpu.make_async_copy(ref, ref, sem.at[it, stage]).wait()

    def send_sums(it):
        for copy in scatter_copies(it):
            copy.start()

    def refit(it):
        await_bytes(0, it, recv_sem)
        mine = pl.ds(me * share, share)
        total = part[it, mine] + jnp.sum(rs_recv[it], axis=0)
        mean = total[:, 0] / elites
        deviation = jnp.sqrt(jnp.maximum(total[:, 1] / elites - mean * mean, 0.0))
        mixed = MOMENTUM * spr[mine] + (1.0 - MOMENTUM) * deviation
        lane = lax.broadcasted_iota(jnp.int32, (SUB, LANES), 1)
        sub = lax.broadcasted_iota(jnp.int32, (SUB, LANES), 0)
        row = jnp.zeros((SUB, LANES), jnp.float32)
        for i in range(share):
            half = lax.rem(me * share + i, halves)
            best = jnp.max(mixed[i], axis=1, keepdims=True)
            row = jnp.maximum(row, jnp.where(lane == half * SUB + sub, best, 0.0))
        row = jnp.max(row, axis=0, keepdims=True)
        p_send[it] = jnp.broadcast_to(row, (SUB, LANES))
        for copy in row_copies(it):
            copy.start()
        ag[it, mine, 0] = MOMENTUM * cen[mine] + (1.0 - MOMENTUM) * mean
        ag[it, mine, 1] = mixed
        for copy in gather_copies(it):
            copy.start()

    def send_peaks(it):
        await_bytes(3, it, recv_sem)
        z_send[it] = jnp.maximum(p_send[it], jnp.max(p_recv[it], axis=0))
        for copy in peak_copies(it):
            copy.start()

    def settle(it):
        await_bytes(2, it, recv_sem)
        own = z_send[it]
        others = z_recv[it]
        peak = jnp.max(jnp.maximum(own, jnp.max(others, axis=0)), axis=1, keepdims=True)
        ratios = own / peak + jnp.sum(others / peak[None], axis=0)
        settled = jnp.sum(ratios, axis=1, keepdims=True) / (env_dev * n_env)
        floor = jnp.broadcast_to(FLOOR_SHARE * peak, (SUB, LANES))
        gain = jnp.broadcast_to(0.5 + settled, (SUB, LANES))
        await_bytes(1, it, recv_sem)
        for unit in range(n_units):
            cen[unit] = ag[it, unit, 0]
            spr[unit] = jnp.maximum(ag[it, unit, 1], floor) * gain

    def rollout(its, low, high):
        bias_h = bi_ref[...] * 0.5
        bias_o = bo_ref[...]

        def steps(tile, states):
            for p in range(per_tile):
                hidden = []
                for it, now in zip(its, states):
                    x = jnp.concatenate([now.astype(jnp.bfloat16), acts[it, tile]], axis=1)
                    h = jnp.dot(x, w_pair[p], preferred_element_type=jnp.float32) + bias_h
                    hidden.append((h * jnp.tanh(h) + h).astype(jnp.bfloat16))
                new = []
                for it, now, hid in zip(its, states, hidden):
                    delta = jnp.dot(hid, wo_ref[...], preferred_element_type=jnp.float32)
                    then = jnp.tanh(now + delta + bias_o)
                    error = then - goals[...]
                    cost[it] += error * error
                    new.append(then)
                states = tuple(new)
            return states

        final = lax.fori_loop(low, high, steps, tuple(state[it] for it in its))
        for it, now in zip(its, final):
            state[it] = now

    def work(pieces):
        for it, low, high in pieces:
            rollout((it,), low * tiles // 20, high * tiles // 20)

    loads[0].wait()
    color(0, rows)
    for it in range(iters):
        make_actions(it)
        if it == 0:
            pl.semaphore_wait(barrier, n_cand - 1 + n_env - 1)
        send_sums(it)
        if it == 0:
            loads[1].wait()
            color(rows, (iters - 1) * rows)
        work(WHILE_SUMS[it])
        refit(it)
        work(WHILE_PEAKS[it])
        send_peaks(it)
        work(WHILE_MOMENTS[it])
        settle(it)

    for tile in range(tiles):
        for h in range(halves):
            at = (slice(h * SUB, (h + 1) * SUB), slice(tile * LANES, (tile + 1) * LANES))
            fmean_ref[at] = cen[tile * halves + h]
            fstd_ref[at] = spr[tile * halves + h]
    lane = lax.broadcasted_iota(jnp.int32, (env_dev, LANES), 1)
    scale = 1.0 / (state_dim * tiles * per_tile)
    for it in range(iters):
        gathered = jnp.zeros((env_dev, LANES), jnp.float32)
        for c in range(cand_dev):
            total = jnp.sum(cost[it, c * env_dev : (c + 1) * env_dev, :], axis=1, keepdims=True)
            gathered = jnp.where(lane == c, total * scale, gathered)
        cost_out[it] = gathered[:, :cand_dev]
    for it in range(iters):
        for stage in range(4):
            await_bytes(stage, it, send_sem)


def shards(
    white,
    mean_init,
    std_init,
    init_state,
    goal_state,
    w_state,
    w_action,
    w_out,
    bias_in,
    bias_out,
    elite_idx,
):
    iters, env_dev, cand_dev, flat = white.shape
    act, hidden = w_action.shape
    state_dim = w_state.shape[0]
    hor_act = mean_init.shape[1]
    n_cand = lax.axis_size("cand")
    n_env = lax.axis_size("env")
    tiles = hor_act // LANES
    halves = env_dev // SUB
    share = -(-tiles * halves // n_cand)
    units = share * n_cand
    rows = env_dev * cand_dev
    out_blocks = hor_act // WIDE
    table_rows = flat + (out_blocks - 1) * WIDE
    dims = (iters, env_dev, cand_dev, act, tiles, units, share, n_cand, n_env, elite_idx.shape[2])
    vmem = pl.BlockSpec(memory_space=pltpu.VMEM)
    f32, bf16 = jnp.float32, jnp.bfloat16
    return pl.pallas_call(
        functools.partial(plan_kernel, dims),
        out_shape=(
            jax.ShapeDtypeStruct((env_dev, hor_act), f32),
            jax.ShapeDtypeStruct((env_dev, hor_act), f32),
            jax.ShapeDtypeStruct((iters, env_dev, cand_dev), f32),
        ),
        in_specs=[pl.BlockSpec(memory_space=pl.ANY)] + [vmem] * 11,
        out_specs=(vmem, vmem, vmem),
        scratch_shapes=[
            pltpu.VMEM((iters * rows, flat), bf16),
            pltpu.VMEM((table_rows, WIDE), bf16),
            pltpu.VMEM((tiles, iters * rows, LANES), f32),
            pltpu.VMEM((iters, tiles, rows, LANES), bf16),
            pltpu.VMEM((LANES // act, state_dim + LANES, hidden), bf16),
            pltpu.VMEM((iters, rows, state_dim), f32),
            pltpu.VMEM((rows, state_dim), f32),
            pltpu.VMEM((iters, rows, LANES), f32),
            pltpu.VMEM((iters, cand_dev, env_dev, LANES), f32),
            pltpu.VMEM((units, SUB, LANES), f32),
            pltpu.VMEM((units, SUB, LANES), f32),
            pltpu.VMEM((iters, units, 2, SUB, LANES), f32),
            pltpu.VMEM((iters, n_cand - 1, share, 2, SUB, LANES), f32),
            pltpu.VMEM((iters, units, 2, SUB, LANES), f32),
            pltpu.VMEM((iters, SUB, LANES), f32),
            pltpu.VMEM((iters, n_env - 1, SUB, LANES), f32),
            pltpu.VMEM((iters, SUB, LANES), f32),
            pltpu.VMEM((iters, n_cand - 1, SUB, LANES), f32),
            pltpu.SemaphoreType.DMA((2,)),
            pltpu.SemaphoreType.DMA((iters, 4)),
            pltpu.SemaphoreType.DMA((iters, 4)),
        ],
        compiler_params=pltpu.CompilerParams(collective_id=0, has_side_effects=True),
    )(
        white.reshape(iters * rows, flat),
        mean_init,
        std_init,
        init_state,
        goal_state,
        w_state,
        w_action,
        w_out,
        bias_in.reshape(1, hidden),
        bias_out.reshape(1, state_dim),
        jnp.swapaxes(elite_idx, 0, 1),
        color_rows(flat // act, act).reshape(-1, WIDE // act, WIDE),
    )


def solution(mesh):
    in_specs = (
        P(None, "env", "cand", None),
        P("env", None),
        P("env", None),
        P("env", None),
        P("env", None),
        P(),
        P(),
        P(),
        P(),
        P(),
        P("env", None, None),
    )
    out_specs = (P("env", None), P("env", None), P(None, "env", "cand"))
    return jax.shard_map(shards, mesh=mesh, in_specs=in_specs, out_specs=out_specs, check_vma=False)
```

profile of v0, /device:TPU:0, one launch (start us, length us, event | category | flops | bytes accessed | tf_op | source)
XLA Modules:
  0.0 70.3 jit_solution(6830687215167376159)
XLA Ops:
  0.6 1.4 %copy.15 = s32[16,3,6]{2,0,1:T(8,128)} copy(s32[16,3,6]{0,2,1:T(8,128)} %param.22) | data formatting | bytes 2304 | tf_op args[10]
  2.0 63.7 %shard_map.139 = (f32[16,2560]{1,0:T(8,128)}, f32[16,2560]{1,0:T(8,128)}, f32[3,16,8]{2,1,0:T(8,128)}) custom-call(bf16[384,4096]{1,0:T(8,128)(2,1)} %bitcast.4, f32[16,2560]{1,0:T(8,128)} %mean_ref.1, f32[16,2560]{1,0:T(8,128)} %std_ref.1, f32[16,128]{1,0:T(8,128)} %start_ref.1, f32[16,128]{1,0:T(8,128)} %goal_ref.1, bf16[128,512]{1,0:T(8,128)(2,1)} %ws_ref.1, ...), custom_call_target="tpu_custom_call" | custom-call | tf_op jit(solution)/shard_map/pallas_call | solution.py:378
  65.7 1.4 %copy.16 = f32[3,16,8]{1,2,0:T(8,128)} copy(f32[3,16,8]{2,1,0:T(8,128)} %get-tuple-element.5) | data formatting | bytes 3072 | tf_op jit(solution)/shard_map/pallas_call | solution.py:378
  67.1 1.6 %copy.19 = f32[16,2560]{1,0:T(8,128)} copy(f32[16,2560]{1,0:T(8,128)} %get-tuple-element.9) | data formatting | bytes 327680
  68.7 1.6 %copy.20 = f32[16,2560]{1,0:T(8,128)} copy(f32[16,2560]{1,0:T(8,128)} %get-tuple-element.10) | data formatting | bytes 327680
where the time goes:
time: 70.6 us; the launch traced here: 70.3 us
  Pallas kernels  63.7 us (90%)
  local copies, waits for them, and re-layouts  6 us (8%)
    pallas_call x1, Pallas kernels, shards(): pl.pallas_call(functools.partial(plan_kernel, dims), out_shape=(jax.Shape...  63.7 us
    unnamed x3, local copies, waits for them, and re-layouts  4.59 us

commit v1 on v0

v1 whole, which is shorter than its diff:
```python
import functools

import jax
import jax.numpy as jnp
import numpy as np
from jax import lax
from jax.experimental import pallas as pl
from jax.experimental.pallas import tpu as pltpu
from jax.sharding import PartitionSpec as P

BETA_EXP = 2.5
MOMENTUM = 0.1
FLOOR_SHARE = 0.1
ACT_COST = 0.1
MESH = pl.DeviceIdType.MESH
LANES = 128
WIDE = 256
SUB = 8

WHILE_SUMS = ((), ((((0, 9), (1, 0)), 9),), ((((2, 0), (1, 16)), 4), (((2, 4),), 8)))
WHILE_PEAKS = ((((((0, 0),), 9)),), ((((0, 18), (1, 9)), 2), (((1, 11),), 5)), ((((2, 12),), 8),))


def color_rows(length, act):
    freqs = np.arange(length // 2 + 1)
    scale = (np.maximum(freqs, 1) / length) ** (-BETA_EXP / 2)
    kernel = np.fft.irfft(scale, n=length)
    kernel = kernel / np.sqrt(np.sum(kernel * kernel))
    q = WIDE // act
    row = np.arange(length)
    lane_step = np.arange(WIDE) // act
    shift = (q * (row // q))[:, None] + lane_step[None, :] - (row % q)[:, None]
    return jnp.asarray(kernel[shift % length], dtype=jnp.bfloat16).astype(jnp.float32)


def plan_kernel(
    dims,
    white_hbm,
    mean_hbm,
    std_hbm,
    start_hbm,
    goal_hbm,
    ws_hbm,
    wa_hbm,
    wo_hbm,
    bi_hbm,
    bo_hbm,
    elite_hbm,
    color_hbm,
    fmean_ref,
    fstd_ref,
    cost_out,
    white,
    mean_ref,
    std_ref,
    start_ref,
    goal_ref,
    ws_ref,
    wa_ref,
    wo_ref,
    bi_ref,
    bo_ref,
    elite_ref,
    color_ref,
    table,
    noise,
    acts,
    w_pair,
    state,
    goals,
    cost,
    member,
    cen,
    spr,
    part,
    rs_recv,
    ag,
    z_send,
    z_recv,
    copy_sem,
    send_sem,
    recv_sem,
):
    iters, env_dev, cand_dev, act, tiles, units, share, n_cand, n_env, elites = dims
    rows = env_dev * cand_dev
    state_dim = start_ref.shape[1]
    halves = env_dev // SUB
    n_units = tiles * halves
    n_all = n_cand * n_env
    length_blocks = white.shape[1] // WIDE
    out_blocks = tiles * LANES // WIDE
    low_block = length_blocks - out_blocks + 1
    per_tile = LANES // act
    me = lax.axis_index("cand")
    me_env = lax.axis_index("env")

    pairs = (
        (color_hbm, color_ref),
        (white_hbm.at[pl.ds(0, rows)], white.at[pl.ds(0, rows)]),
        (elite_hbm, elite_ref),
        (mean_hbm, mean_ref),
        (std_hbm, std_ref),
        (start_hbm, start_ref),
        (goal_hbm, goal_ref),
        (ws_hbm, ws_ref),
        (wa_hbm, wa_ref),
        (wo_hbm, wo_ref),
        (bi_hbm, bi_ref),
        (bo_hbm, bo_ref),
        (
            white_hbm.at[pl.ds(rows, (iters - 1) * rows)],
            white.at[pl.ds(rows, (iters - 1) * rows)],
        ),
    )
    loads = [
        pltpu.make_async_copy(src, dst, copy_sem.at[at]) for at, (src, dst) in enumerate(pairs)
    ]
    for load in loads:
        load.start()

    def peer_of(k):
        return {
            "env": lax.rem(me_env + k // n_cand, n_env),
            "cand": lax.rem(me + k % n_cand, n_cand),
        }

    def every_peer(visit):
        if n_all <= 64:
            for k in range(1, n_all):
                visit(k)
        else:
            lax.fori_loop(1, n_all, lambda k, carry: (visit(k), carry)[1], 0)

    barrier = pltpu.get_barrier_semaphore()
    every_peer(
        lambda k: pl.semaphore_signal(barrier, inc=1, device_id=peer_of(k), device_id_type=MESH)
    )

    q = WIDE // act
    eye = (
        lax.broadcasted_iota(jnp.int32, (act, WIDE), 0)
        == lax.broadcasted_iota(jnp.int32, (act, WIDE), 1) % act
    )

    def build(block, carry):
        shift = lax.rem(2 * length_blocks - (block + low_block), length_blocks)
        for j in range(q):
            line = color_ref[shift, j : j + 1, :]
            piece = jnp.where(eye, line, 0.0).astype(jnp.bfloat16)
            table[pl.ds(pl.multiple_of(block * WIDE + j * act, act), act), :] = piece
        return carry

    loads[0].wait()
    lax.fori_loop(0, table.shape[0] // WIDE, build, 0)

    for load in loads[2:-1]:
        load.wait()
    w_pair[...] = jnp.zeros_like(w_pair)
    for p in range(per_tile):
        w_pair[p, :state_dim, :] = ws_ref[...] * jnp.bfloat16(0.5)
        w_pair[p, state_dim + p * act : state_dim + (p + 1) * act, :] = wa_ref[...] * jnp.bfloat16(0.5)
    diagonal = lax.broadcasted_iota(jnp.int32, (env_dev, env_dev), 0) == lax.broadcasted_iota(
        jnp.int32, (env_dev, env_dev), 1
    )
    for it in range(iters):
        own = elite_ref[it]
        for c in range(cand_dev):
            hit = (own == me * cand_dev + c).astype(jnp.float32)
            hit = jnp.sum(hit, axis=0, keepdims=True)
            hit = jnp.sum(jnp.where(diagonal, hit, 0.0), axis=1, keepdims=True)
            member[it, c] = jnp.broadcast_to(hit, (env_dev, LANES))
    for c in range(cand_dev):
        spot = slice(c * env_dev, (c + 1) * env_dev)
        goals[spot, :] = goal_ref[...]
        for it in range(iters):
            state[it, spot, :] = start_ref[...]
    cost[...] = jnp.zeros_like(cost)
    if units > n_units:
        cen[...] = jnp.zeros_like(cen)
        spr[...] = jnp.zeros_like(spr)
        part[...] = jnp.zeros_like(part)
    for tile in range(tiles):
        for h in range(halves):
            at = (slice(h * SUB, (h + 1) * SUB), slice(tile * LANES, (tile + 1) * LANES))
            cen[tile * halves + h] = mean_ref[at]
            spr[tile * halves + h] = std_ref[at]

    def color(first, size):
        spot = slice(first, first + size)
        group = 2 if out_blocks % 2 == 0 else 1

        def one(step, carry):
            for g in range(group):
                block = step * group + g
                start = pl.multiple_of((out_blocks - 1 - block) * WIDE, WIDE)
                band = table[pl.ds(start, white.shape[1]), :]
                out = jnp.dot(white[spot, :], band, preferred_element_type=jnp.float32)
                for p in range(WIDE // LANES):
                    noise[block * (WIDE // LANES) + p, spot, :] = out[:, p * LANES : (p + 1) * LANES]
            return carry

        lax.fori_loop(0, out_blocks // group, one, 0)

    act_weight = ACT_COST * state_dim / act

    def model(it, unit, scales):
        if it == 0:
            return cen[unit], spr[unit]
        floor, gain = scales
        return ag[it - 1, unit, 0], jnp.maximum(ag[it - 1, unit, 1], floor) * gain

    def make_actions(it, scales):
        def one(tile, carry):
            fitted = [model(it, tile * halves + h, scales) for h in range(halves)]
            center = jnp.concatenate([f[0] for f in fitted], axis=0)
            spread = jnp.concatenate([f[1] for f in fitted], axis=0)
            sums = jnp.zeros((env_dev, LANES), jnp.float32)
            squares = jnp.zeros((env_dev, LANES), jnp.float32)
            for c in range(cand_dev):
                drawn = noise[tile, pl.ds(it * rows + c, env_dev, stride=cand_dev), :]
                action = jnp.clip(center + spread * drawn, -1.0, 1.0)
                spot = slice(c * env_dev, (c + 1) * env_dev)
                acts[it, tile, spot, :] = action.astype(jnp.bfloat16)
                chosen = member[it, c] * action
                square = action * action
                sums = sums + chosen
                squares = squares + chosen * action
                cost[it, spot, :] += act_weight * square
            sums = sums.reshape(halves, SUB, LANES)
            squares = squares.reshape(halves, SUB, LANES)
            for h in range(halves):
                part[it, tile * halves + h, 0] = sums[h]
                part[it, tile * halves + h, 1] = squares[h]
            return carry

        lax.fori_loop(0, tiles, one, 0)

    def scatter_copies(it):
        for o in range(1, n_cand):
            peer = lax.rem(me + o, n_cand)
            yield pltpu.make_async_remote_copy(
                src_ref=part.at[it, pl.ds(peer * share, share)],
                dst_ref=rs_recv.at[it, o - 1],
                send_sem=send_sem.at[it, 0],
                recv_sem=recv_sem.at[it, 0],
                device_id={"cand": peer},
                device_id_type=MESH,
            )

    def gather_copies(it):
        mine = ag.at[it, pl.ds(me * share, share)]
        for o in range(1, n_cand):
            yield pltpu.make_async_remote_copy(
                src_ref=mine,
                dst_ref=mine,
                send_sem=send_sem.at[it, 1],
                recv_sem=recv_sem.at[it, 1],
                device_id={"cand": lax.rem(me + o, n_cand)},
                device_id_type=MESH,
            )

    def send_peaks(it):
        every_peer(
            lambda k: pltpu.make_async_remote_copy(
                src_ref=z_send.at[it],
                dst_ref=z_recv.at[it, k],
                send_sem=send_sem.at[it, 2],
                recv_sem=recv_sem.at[it, 2],
                device_id=peer_of(k),
                device_id_type=MESH,
            ).start()
        )

    def await_bytes(stage, it, sem):
        others = (n_cand - 1) * share
        ref = (rs_recv.at[it], ag.at[it, pl.ds(0, others)], z_recv.at[it, pl.ds(1, n_all - 1)])[stage]
        pltpu.make_async_copy(ref, ref, sem.at[it, stage]).wait()

    def send_sums(it):
        for copy in scatter_copies(it):
            copy.start()

    def refit(it, scales):
        await_bytes(0, it, recv_sem)
        mine = pl.ds(me * share, share)
        total = part[it, mine] + jnp.sum(rs_recv[it], axis=0)
        mean = total[:, 0] / elites
        deviation = jnp.sqrt(jnp.maximum(total[:, 1] / elites - mean * mean, 0.0))
        center, spread = model(it, mine, scales)
        mixed = MOMENTUM * spread + (1.0 - MOMENTUM) * deviation
        lane = lax.broadcasted_iota(jnp.int32, (SUB, LANES), 1)
        sub = lax.broadcasted_iota(jnp.int32, (SUB, LANES), 0)
        row = jnp.zeros((SUB, LANES), jnp.float32)
        for i in range(share):
            half = lax.rem(me * share + i, halves)
            best = jnp.max(mixed[i], axis=1, keepdims=True)
            row = jnp.maximum(row, jnp.where(lane == half * SUB + sub, best, 0.0))
        row = jnp.max(row, axis=0, keepdims=True)
        z_send[it] = row
        z_recv[it, 0] = row
        send_peaks(it)
        ag[it, mine, 0] = MOMENTUM * center + (1.0 - MOMENTUM) * mean
        ag[it, mine, 1] = mixed
        for copy in gather_copies(it):
            copy.start()

    def settle(it):
        await_bytes(2, it, recv_sem)
        peaks = jnp.max(z_recv[it].reshape(n_env, n_cand, 1, LANES), axis=1)
        peak = jnp.max(jnp.max(peaks, axis=0), axis=1, keepdims=True)
        settled = jnp.sum(jnp.sum(peaks, axis=0), axis=1, keepdims=True) / peak / (env_dev * n_env)
        floor = jnp.broadcast_to(FLOOR_SHARE * peak, (SUB, LANES))
        gain = jnp.broadcast_to(0.5 + settled, (SUB, LANES))
        await_bytes(1, it, recv_sem)
        return floor, gain

    def rollout(chains, count):
        bias_h = bi_ref[...] * 0.5
        bias_o = bo_ref[...]
        its = [it for it, _ in chains]

        def steps(i, carry):
            for p in range(per_tile):
                hidden = []
                for it, low in chains:
                    x = jnp.concatenate([state[it].astype(jnp.bfloat16), acts[it, low + i]], axis=1)
                    h = jnp.dot(x, w_pair[p], preferred_element_type=jnp.float32) + bias_h
                    hidden.append((h * jnp.tanh(h) + h).astype(jnp.bfloat16))
                for it, hid in zip(its, hidden):
                    delta = jnp.dot(hid, wo_ref[...], preferred_element_type=jnp.float32)
                    then = jnp.tanh(state[it] + delta + bias_o)
                    error = then - goals[...]
                    cost[it] += error * error
                    state[it] = then
            return carry

        lax.fori_loop(0, count, steps, 0)

    def work(groups):
        for chains, count in groups:
            rollout(
                tuple((it, low * tiles // 20) for it, low in chains), count * tiles // 20
            )

    loads[1].wait()
    color(0, rows)
    scales = None
    for it in range(iters):
        make_actions(it, scales)
        if it == 0:
            pl.semaphore_wait(barrier, n_all - 1)
        send_sums(it)
        if it == 0:
            loads[-1].wait()
            color(rows, (iters - 1) * rows)
        work(WHILE_SUMS[it])
        refit(it, scales)
        work(WHILE_PEAKS[it])
        scales = settle(it)

    for tile in range(tiles):
        for h in range(halves):
            at = (slice(h * SUB, (h + 1) * SUB), slice(tile * LANES, (tile + 1) * LANES))
            fmean_ref[at], fstd_ref[at] = model(iters, tile * halves + h, scales)
    scale = 1.0 / (state_dim * tiles * per_tile)
    for it in range(iters):
        for c in range(cand_dev):
            total = jnp.sum(cost[it, c * env_dev : (c + 1) * env_dev, :], axis=1, keepdims=True)
            line = jnp.sum(jnp.where(diagonal, total * scale, 0.0), axis=0, keepdims=True)
            cost_out[it, c : c + 1, :] = line
    for it in range(iters):
        for stage in range(3):
            await_bytes(stage, it, send_sem)


def shards(
    white,
    mean_init,
    std_init,
    init_state,
    goal_state,
    w_state,
    w_action,
    w_out,
    bias_in,
    bias_out,
    elite_idx,
):
    iters, env_dev, cand_dev, flat = white.shape
    act, hidden = w_action.shape
    state_dim = w_state.shape[0]
    hor_act = mean_init.shape[1]
    n_cand = lax.axis_size("cand")
    n_env = lax.axis_size("env")
    tiles = hor_act // LANES
    halves = env_dev // SUB
    share = -(-tiles * halves // n_cand)
    units = share * n_cand
    rows = env_dev * cand_dev
    out_blocks = hor_act // WIDE
    table_rows = flat + (out_blocks - 1) * WIDE
    dims = (iters, env_dev, cand_dev, act, tiles, units, share, n_cand, n_env, elite_idx.shape[2])
    hbm = pl.BlockSpec(memory_space=pl.ANY)
    vmem = pl.BlockSpec(memory_space=pltpu.VMEM)
    f32, bf16 = jnp.float32, jnp.bfloat16
    outs = (
        ((env_dev, hor_act), f32),
        ((env_dev, hor_act), f32),
        ((iters, cand_dev, env_dev), f32),
    )
    operands = (
        white.reshape(iters * rows, flat),
        mean_init,
        std_init,
        init_state,
        goal_state,
        w_state,
        w_action,
        w_out,
        bias_in.reshape(1, hidden),
        bias_out.reshape(1, state_dim),
        jnp.transpose(elite_idx, (1, 2, 0)),
        color_rows(flat // act, act).reshape(-1, WIDE // act, WIDE),
    )
    fmean, fstd, cost = pl.pallas_call(
        functools.partial(plan_kernel, dims),
        out_shape=tuple(pltpu.VMEM(shape, kind) for shape, kind in outs),
        in_specs=[hbm] * len(operands),
        out_specs=(vmem, vmem, vmem),
        scratch_shapes=[
            *(pltpu.VMEM(operand.shape, operand.dtype) for operand in operands),
            pltpu.VMEM((table_rows, WIDE), bf16),
            pltpu.VMEM((tiles, iters * rows, LANES), f32),
            pltpu.VMEM((iters, tiles, rows, LANES), bf16),
            pltpu.VMEM((LANES // act, state_dim + LANES, hidden), bf16),
            pltpu.VMEM((iters, rows, state_dim), f32),
            pltpu.VMEM((rows, state_dim), f32),
            pltpu.VMEM((iters, rows, LANES), f32),
            pltpu.VMEM((iters, cand_dev, env_dev, LANES), f32),
            pltpu.VMEM((units, SUB, LANES), f32),
            pltpu.VMEM((units, SUB, LANES), f32),
            pltpu.VMEM((iters, units, 2, SUB, LANES), f32),
            pltpu.VMEM((iters, n_cand - 1, share, 2, SUB, LANES), f32),
            pltpu.VMEM((iters, units, 2, SUB, LANES), f32),
            pltpu.VMEM((iters, 1, LANES), f32),
            pltpu.VMEM((iters, n_cand * n_env, 1, LANES), f32),
            pltpu.SemaphoreType.DMA((len(operands) + 1,)),
            pltpu.SemaphoreType.DMA((iters, 3)),
            pltpu.SemaphoreType.DMA((iters, 3)),
        ],
        compiler_params=pltpu.CompilerParams(collective_id=0, has_side_effects=True),
    )(*operands)
    return fmean, fstd, jnp.swapaxes(cost, 1, 2)


def solution(mesh):
    in_specs = (
        P(None, "env", "cand", None),
        P("env", None),
        P("env", None),
        P("env", None),
        P("env", None),
        P(),
        P(),
        P(),
        P(),
        P(),
        P("env", None, None),
    )
    out_specs = (P("env", None), P("env", None), P(None, "env", "cand"))
    return jax.shard_map(shards, mesh=mesh, in_specs=in_specs, out_specs=out_specs, check_vma=False)
```

time: 70.6 us -> 50.6 us (0.72)
  Pallas kernels: 63.7 us -> 47.9 us
  local copies, waits for them, and re-layouts: 6 us -> 1.93 us
    pallas_call x1, Pallas kernels: 63.7 us -> 47.9 us  [shards(): pl.pallas_call(functools.partial(plan_kernel, dims), out_shape=tuple((plt...]
    unnamed x3, local copies, waits for them, and re-layouts: 4.59 us -> 1.93 us
    pallas_call x1 -> x0, local copies, waits for them, and re-layouts: 1.41 us -> none  [shards(): pl.pallas_call(functools.partial(plan_kernel, dims), out_shape=(jax.Shape...]
where the time goes in v1:
time: 50.6 us; the launch traced here: 50.5 us
  Pallas kernels  47.9 us (95%)
  local copies, waits for them, and re-layouts  1.93 us (4%)
  between operations  0.64 us (1%)
    pallas_call x1, Pallas kernels, shards(): pl.pallas_call(functools.partial(plan_kernel, dims), out_shape=tuple((plt...  47.9 us
    unnamed x3, local copies, waits for them, and re-layouts  1.93 us

profile of v1, /device:TPU:0, one launch (start us, length us, event | category | flops | bytes accessed | tf_op | source)
XLA Modules:
  0.0 50.5 jit_solution(9649872527510267041)
XLA Ops:
  0.6 47.9 %shard_map.139 = (f32[16,2560]{1,0:T(8,128)S(1)}, f32[16,2560]{1,0:T(8,128)S(1)}, f32[3,8,16]{2,1,0:T(8,128)S(1)}) custom-call(bf16[384,4096]{1,0:T(8,128)(2,1)} %bitcast.6, f32[16,2560]{1,0:T(8,128)} %mean_hbm.1, f32[16,2560]{1,0:T(8,128)} %std_hbm.1, f32[16,128]{1,0:T(8,128)} %start_hbm.1, f32[16,128]{1,0:T(8,128)} %goal_hbm.1, bf16[128,512]{1,0:T(8,128)(2,1)} %ws_hbm.1, ...), custom_call_target="tpu_custom_call" | custom-call | tf_op jit(solution)/shard_map/pallas_call | solution.py:425
  48.5 0.7 %copy.18 = f32[16,2560]{1,0:T(8,128)} copy(f32[16,2560]{1,0:T(8,128)S(1)} %get-tuple-element.9) | data formatting | bytes 327680
  49.2 0.6 %copy.20 = f32[3,16,8]{1,2,0:T(8,128)} copy(f32[3,16,8]{1,2,0:T(8,128)S(1)} %bitcast.5) | data formatting | bytes 3072
  49.8 0.7 %copy.19 = f32[16,2560]{1,0:T(8,128)} copy(f32[16,2560]{1,0:T(8,128)S(1)} %get-tuple-element.10) | data formatting | bytes 327680

commit v2 on v1

--- a/solution.py
+++ b/solution.py
@@ -17,8 +17,18 @@
 WIDE = 256
 SUB = 8
 
-WHILE_SUMS = ((), ((((0, 9), (1, 0)), 9),), ((((2, 0), (1, 16)), 4), (((2, 4),), 8)))
-WHILE_PEAKS = ((((((0, 0),), 9)),), ((((0, 18), (1, 9)), 2), (((1, 11),), 5)), ((((2, 12),), 8),))
+TRIPS = 10
+WHILE_EARLY = (
+    ((((0, 0),), 2, 1, (1, 0)),),
+    ((((0, 6), (1, 0)), 2, 1, (2, 0)),),
+    ((((2, 0), (1, 6)), 2, 2, None),),
+)
+WHILE_LATE = ((), (), ())
+WHILE_PEAKS = (
+    ((((0, 2),), 3, 1, (1, 4)), (((0, 5),), 1, 1, None)),
+    ((((0, 8), (1, 2)), 2, 1, (2, 4)), (((1, 4),), 1, 1, (2, 8)), (((1, 5),), 1, 1, None)),
+    ((((2, 4),), 3, 2, None),),
+)
 
 
 def color_rows(length, act):
@@ -115,7 +125,7 @@
     loads = [
         pltpu.make_async_copy(src, dst, copy_sem.at[at]) for at, (src, dst) in enumerate(pairs)
     ]
-    for load in loads:
+    for load in loads[:-1]:
         load.start()
 
     def peer_of(k):
@@ -142,64 +152,93 @@
         == lax.broadcasted_iota(jnp.int32, (act, WIDE), 1) % act
     )
 
-    def build(block, carry):
+    def build(places, block, carry):
         shift = lax.rem(2 * length_blocks - (block + low_block), length_blocks)
         for j in range(q):
             line = color_ref[shift, j : j + 1, :]
             piece = jnp.where(eye, line, 0.0).astype(jnp.bfloat16)
-            table[pl.ds(pl.multiple_of(block * WIDE + j * act, act), act), :] = piece
+            for place in places:
+                start = pl.multiple_of((block + place) * WIDE + j * act, act)
+                table[pl.ds(start, act), :] = piece
         return carry
 
-    loads[0].wait()
-    lax.fori_loop(0, table.shape[0] // WIDE, build, 0)
-
-    for load in loads[2:-1]:
-        load.wait()
-    w_pair[...] = jnp.zeros_like(w_pair)
-    for p in range(per_tile):
-        w_pair[p, :state_dim, :] = ws_ref[...] * jnp.bfloat16(0.5)
-        w_pair[p, state_dim + p * act : state_dim + (p + 1) * act, :] = wa_ref[...] * jnp.bfloat16(0.5)
     diagonal = lax.broadcasted_iota(jnp.int32, (env_dev, env_dev), 0) == lax.broadcasted_iota(
         jnp.int32, (env_dev, env_dev), 1
     )
-    for it in range(iters):
+
+    def mark_elites(it):
         own = elite_ref[it]
         for c in range(cand_dev):
             hit = (own == me * cand_dev + c).astype(jnp.float32)
             hit = jnp.sum(hit, axis=0, keepdims=True)
             hit = jnp.sum(jnp.where(diagonal, hit, 0.0), axis=1, keepdims=True)
             member[it, c] = jnp.broadcast_to(hit, (env_dev, LANES))
-    for c in range(cand_dev):
-        spot = slice(c * env_dev, (c + 1) * env_dev)
-        goals[spot, :] = goal_ref[...]
-        for it in range(iters):
-            state[it, spot, :] = start_ref[...]
-    cost[...] = jnp.zeros_like(cost)
-    if units > n_units:
-        cen[...] = jnp.zeros_like(cen)
-        spr[...] = jnp.zeros_like(spr)
-        part[...] = jnp.zeros_like(part)
-    for tile in range(tiles):
-        for h in range(halves):
-            at = (slice(h * SUB, (h + 1) * SUB), slice(tile * LANES, (tile + 1) * LANES))
-            cen[tile * halves + h] = mean_ref[at]
-            spr[tile * halves + h] = std_ref[at]
-
-    def color(first, size):
-        spot = slice(first, first + size)
-        group = 2 if out_blocks % 2 == 0 else 1
-
+
+    def set_first():
+        for load in loads[2:5]:
+            load.wait()
+        mark_elites(0)
+        cost[...] = jnp.zeros_like(cost)
+        if units > n_units:
+            cen[...] = jnp.zeros_like(cen)
+            spr[...] = jnp.zeros_like(spr)
+            part[...] = jnp.zeros_like(part)
+        for tile in range(tiles):
+            for h in range(halves):
+                at = (slice(h * SUB, (h + 1) * SUB), slice(tile * LANES, (tile + 1) * LANES))
+                cen[tile * halves + h] = mean_ref[at]
+                spr[tile * halves + h] = std_ref[at]
+
+    def set_rest():
+        for load in loads[5:]:
+            load.wait()
+        w_pair[...] = jnp.zeros_like(w_pair)
+        for p in range(per_tile):
+            w_pair[p, :state_dim, :] = ws_ref[...] * jnp.bfloat16(0.5)
+            w_pair[p, state_dim + p * act : state_dim + (p + 1) * act, :] = wa_ref[...] * jnp.bfloat16(0.5)
+        for it in range(1, iters):
+            mark_elites(it)
+        for c in range(cand_dev):
+            spot = slice(c * env_dev, (c + 1) * env_dev)
+            goals[spot, :] = goal_ref[...]
+            for it in range(iters):
+                state[it, spot, :] = start_ref[...]
+
+    n_blocks = table.shape[0] // WIDE
+    twice = min(max(n_blocks - length_blocks, 0), length_blocks)
+    loads[0].wait()
+    lax.fori_loop(0, twice, functools.partial(build, (0, length_blocks)), 0)
+    lax.fori_loop(twice, min(length_blocks, n_blocks), functools.partial(build, (0,)), 0)
+    loads[-1].start()
+    set_first()
+
+    def color_block(it, block):
+        spot = pl.ds(it * rows, rows)
+        start = pl.multiple_of((out_blocks - 1 - block) * WIDE, WIDE)
+        band = table[pl.ds(start, white.shape[1]), :]
+        out = jnp.dot(white[spot, :], band, preferred_element_type=jnp.float32)
+        for p in range(WIDE // LANES):
+            noise[block * (WIDE // LANES) + p, spot, :] = out[:, p * LANES : (p + 1) * LANES]
+
+    def color_piece(it, block, piece, pieces):
+        spot = pl.ds(it * rows, rows)
+        width = white.shape[1] // pieces
+        start = pl.multiple_of((out_blocks - 1 - block) * WIDE + piece * width, WIDE)
+        band = table[pl.ds(start, width), :]
+        taken = white[spot, piece * width : (piece + 1) * width]
+        out = jnp.dot(taken, band, preferred_element_type=jnp.float32)
+        for p in range(WIDE // LANES):
+            half = out[:, p * LANES : (p + 1) * LANES]
+            at = block * (WIDE // LANES) + p
+            noise[at, spot, :] = half if piece == 0 else noise[at, spot, :] + half
+
+    def color(it, first, count, group):
         def one(step, carry):
             for g in range(group):
-                block = step * group + g
-                start = pl.multiple_of((out_blocks - 1 - block) * WIDE, WIDE)
-                band = table[pl.ds(start, white.shape[1]), :]
-                out = jnp.dot(white[spot, :], band, preferred_element_type=jnp.float32)
-                for p in range(WIDE // LANES):
-                    noise[block * (WIDE // LANES) + p, spot, :] = out[:, p * LANES : (p + 1) * LANES]
+                color_block(it, first + step * group + g)
             return carry
 
-        lax.fori_loop(0, out_blocks // group, one, 0)
+        lax.fori_loop(0, count // group, one, 0)
 
     act_weight = ACT_COST * state_dim / act
 
@@ -209,7 +248,7 @@
         floor, gain = scales
         return ag[it - 1, unit, 0], jnp.maximum(ag[it - 1, unit, 1], floor) * gain
 
-    def make_actions(it, scales):
+    def make_actions(it, scales, first, count):
         def one(tile, carry):
             fitted = [model(it, tile * halves + h, scales) for h in range(halves)]
             center = jnp.concatenate([f[0] for f in fitted], axis=0)
@@ -233,144 +272,192 @@
                 part[it, tile * halves + h, 1] = squares[h]
             return carry
 
-        lax.fori_loop(0, tiles, one, 0)
-
-    def scatter_copies(it):
-        for o in range(1, n_cand):
-            peer = lax.rem(me + o, n_cand)
-            yield pltpu.make_async_remote_copy(
-                src_ref=part.at[it, pl.ds(peer * share, share)],
-                dst_ref=rs_recv.at[it, o - 1],
-                send_sem=send_sem.at[it, 0],
-                recv_sem=recv_sem.at[it, 0],
+        lax.fori_loop(first, first + count, one, 0)
+
+    parts = 2 if units == n_units and n_cand % 2 == 0 and out_blocks % 2 == 0 else 1
+    crowd = n_cand // parts
+    near = me // crowd
+
+    lots = ((0, share // 2), (share // 2, share - share // 2)) if share > 1 else ((0, share),)
+    sums_stage, means_stage, peaks_stage = 0, len(lots), 2 * len(lots)
+
+    def send_sums(it, part_at, far, lot):
+        low, size = lots[lot]
+        for o in range(0 if far else 1, crowd):
+            peer = part_at * crowd + lax.rem(lax.rem(me, crowd) + o, crowd)
+            pltpu.make_async_remote_copy(
+                src_ref=part.at[it, pl.ds(peer * share + low, size)],
+                dst_ref=rs_recv.at[it, o if far else n_cand - crowd + o - 1, pl.ds(low, size)],
+                send_sem=send_sem.at[it, sums_stage + lot],
+                recv_sem=recv_sem.at[it, sums_stage + lot],
                 device_id={"cand": peer},
                 device_id_type=MESH,
-            )
-
-    def gather_copies(it):
-        mine = ag.at[it, pl.ds(me * share, share)]
+            ).start()
+
+    def send_means(it, lot):
+        low, size = lots[lot]
+        mine = ag.at[it, pl.ds(me * share + low, size)]
         for o in range(1, n_cand):
-            yield pltpu.make_async_remote_copy(
+            pltpu.make_async_remote_copy(
                 src_ref=mine,
                 dst_ref=mine,
-                send_sem=send_sem.at[it, 1],
-                recv_sem=recv_sem.at[it, 1],
+                send_sem=send_sem.at[it, means_stage + lot],
+                recv_sem=recv_sem.at[it, means_stage + lot],
                 device_id={"cand": lax.rem(me + o, n_cand)},
                 device_id_type=MESH,
-            )
+            ).start()
 
     def send_peaks(it):
         every_peer(
             lambda k: pltpu.make_async_remote_copy(
                 src_ref=z_send.at[it],
                 dst_ref=z_recv.at[it, k],
-                send_sem=send_sem.at[it, 2],
-                recv_sem=recv_sem.at[it, 2],
+                send_sem=send_sem.at[it, peaks_stage],
+                recv_sem=recv_sem.at[it, peaks_stage],
                 device_id=peer_of(k),
                 device_id_type=MESH,
             ).start()
         )
 
     def await_bytes(stage, it, sem):
-        others = (n_cand - 1) * share
-        ref = (rs_recv.at[it], ag.at[it, pl.ds(0, others)], z_recv.at[it, pl.ds(1, n_all - 1)])[stage]
+        if stage == peaks_stage:
+            ref = z_recv.at[it, pl.ds(1, n_all - 1)]
+        elif stage < means_stage:
+            low, size = lots[stage]
+            ref = rs_recv.at[it, pl.ds(0, n_cand - 1), pl.ds(low, size)]
+        else:
+            ref = ag.at[it, pl.ds(0, (n_cand - 1) * lots[stage - means_stage][1])]
         pltpu.make_async_copy(ref, ref, sem.at[it, stage]).wait()
 
-    def send_sums(it):
-        for copy in scatter_copies(it):
-            copy.start()
-
-    def refit(it, scales):
-        await_bytes(0, it, recv_sem)
-        mine = pl.ds(me * share, share)
-        total = part[it, mine] + jnp.sum(rs_recv[it], axis=0)
+    def refit(it, scales, lot):
+        low, size = lots[lot]
+        await_bytes(sums_stage + lot, it, recv_sem)
+        mine = pl.ds(me * share + low, size)
+        total = part[it, mine] + jnp.sum(rs_recv[it, :, low : low + size], axis=0)
         mean = total[:, 0] / elites
         deviation = jnp.sqrt(jnp.maximum(total[:, 1] / elites - mean * mean, 0.0))
         center, spread = model(it, mine, scales)
         mixed = MOMENTUM * spread + (1.0 - MOMENTUM) * deviation
+        ag[it, mine, 0] = MOMENTUM * center + (1.0 - MOMENTUM) * mean
+        ag[it, mine, 1] = mixed
         lane = lax.broadcasted_iota(jnp.int32, (SUB, LANES), 1)
         sub = lax.broadcasted_iota(jnp.int32, (SUB, LANES), 0)
         row = jnp.zeros((SUB, LANES), jnp.float32)
-        for i in range(share):
-            half = lax.rem(me * share + i, halves)
+        for i in range(size):
+            half = lax.rem(me * share + low + i, halves)
             best = jnp.max(mixed[i], axis=1, keepdims=True)
             row = jnp.maximum(row, jnp.where(lane == half * SUB + sub, best, 0.0))
         row = jnp.max(row, axis=0, keepdims=True)
+        if lot:
+            row = jnp.maximum(row, z_send[it])
         z_send[it] = row
-        z_recv[it, 0] = row
-        send_peaks(it)
-        ag[it, mine, 0] = MOMENTUM * center + (1.0 - MOMENTUM) * mean
-        ag[it, mine, 1] = mixed
-        for copy in gather_copies(it):
-            copy.start()
+        if lot == len(lots) - 1:
+            z_recv[it, 0] = row
+            send_peaks(it)
+        send_means(it, lot)
 
     def settle(it):
-        await_bytes(2, it, recv_sem)
+        await_bytes(peaks_stage, it, recv_sem)
         peaks = jnp.max(z_recv[it].reshape(n_env, n_cand, 1, LANES), axis=1)
         peak = jnp.max(jnp.max(peaks, axis=0), axis=1, keepdims=True)
         settled = jnp.sum(jnp.sum(peaks, axis=0), axis=1, keepdims=True) / peak / (env_dev * n_env)
         floor = jnp.broadcast_to(FLOOR_SHARE * peak, (SUB, LANES))
         gain = jnp.broadcast_to(0.5 + settled, (SUB, LANES))
-        await_bytes(1, it, recv_sem)
+        for lot in range(len(lots)):
+            await_bytes(means_stage + lot, it, recv_sem)
         return floor, gain
 
-    def rollout(chains, count):
+    per_trip = -(-tiles // TRIPS)
+
+    def rollout(chains, count, span, paint):
         bias_h = bi_ref[...] * 0.5
         bias_o = bo_ref[...]
         its = [it for it, _ in chains]
 
         def steps(i, carry):
-            for p in range(per_tile):
+            pieces = span * per_trip * per_tile
+            for s in range(pieces):
+                tile, p = s // per_tile, s % per_tile
                 hidden = []
                 for it, low in chains:
-                    x = jnp.concatenate([state[it].astype(jnp.bfloat16), acts[it, low + i]], axis=1)
+                    action = acts[it, (low + i * span) * per_trip + tile]
+                    x = jnp.concatenate([state[it].astype(jnp.bfloat16), action], axis=1)
                     h = jnp.dot(x, w_pair[p], preferred_element_type=jnp.float32) + bias_h
                     hidden.append((h * jnp.tanh(h) + h).astype(jnp.bfloat16))
+                if paint is not None:
+                    color_piece(paint[0], paint[1] + i * 2, s, pieces)
                 for it, hid in zip(its, hidden):
                     delta = jnp.dot(hid, wo_ref[...], preferred_element_type=jnp.float32)
-                    then = jnp.tanh(state[it] + delta + bias_o)
+                    then = jnp.tanh((state[it] + bias_o) + delta)
                     error = then - goals[...]
                     cost[it] += error * error
                     state[it] = then
+                if paint is not None:
+                    color_piece(paint[0], paint[1] + i * 2 + 1, s, pieces)
             return carry
 
         lax.fori_loop(0, count, steps, 0)
 
     def work(groups):
-        for chains, count in groups:
-            rollout(
-                tuple((it, low * tiles // 20) for it, low in chains), count * tiles // 20
-            )
+        for chains, count, span, paint in groups:
+            rollout(chains, count, span, paint)
 
     loads[1].wait()
-    color(0, rows)
     scales = None
+    half = out_blocks // parts
+    everything = range(len(lots))
     for it in range(iters):
-        make_actions(it, scales)
+        for k in range(parts):
+            far = k < parts - 1
+            at = lax.rem(near + 1 + k, parts)
+            if it == 0:
+                color(0, at * half, half, half)
+            make_actions(it, scales, at * (tiles // parts), tiles // parts)
+            if it == 0 and k == 0:
+                pl.semaphore_wait(barrier, n_all - 1)
+            for lot in everything if it == 0 or parts == 1 else (0,):
+                send_sums(it, at, far, lot)
+        if it and parts > 1:
+            for k in range(parts):
+                for lot in everything[1:]:
+                    send_sums(it, lax.rem(near + 1 + k, parts), k < parts - 1, lot)
         if it == 0:
-            pl.semaphore_wait(barrier, n_all - 1)
-        send_sums(it)
-        if it == 0:
-            loads[-1].wait()
-            color(rows, (iters - 1) * rows)
-        work(WHILE_SUMS[it])
-        refit(it, scales)
+            set_rest()
+        work(WHILE_EARLY[it])
+        if len(lots) > 1:
+            refit(it, scales, 0)
+        work(WHILE_LATE[it])
+        refit(it, scales, len(lots) - 1)
         work(WHILE_PEAKS[it])
+        if it == iters - 1:
+            scale = 1.0 / (state_dim * tiles * per_tile)
+            for i in range(iters):
+                for c in range(cand_dev):
+                    total = jnp.sum(cost[i, c * env_dev : (c + 1) * env_dev, :], axis=1, keepdims=True)
+                    line = jnp.sum(jnp.where(diagonal, total * scale, 0.0), axis=0, keepdims=True)
+                    cost_out[i, c : c + 1, :] = line
         scales = settle(it)
 
     for tile in range(tiles):
         for h in range(halves):
             at = (slice(h * SUB, (h + 1) * SUB), slice(tile * LANES, (tile + 1) * LANES))
             fmean_ref[at], fstd_ref[at] = model(iters, tile * halves + h, scales)
-    scale = 1.0 / (state_dim * tiles * per_tile)
     for it in range(iters):
-        for c in range(cand_dev):
-            total = jnp.sum(cost[it, c * env_dev : (c + 1) * env_dev, :], axis=1, keepdims=True)
-            line = jnp.sum(jnp.where(diagonal, total * scale, 0.0), axis=0, keepdims=True)
-            cost_out[it, c : c + 1, :] = line
-    for it in range(iters):
-        for stage in range(3):
+        for stage in range(peaks_stage + 1):
             await_bytes(stage, it, send_sem)
+
+
+def store_kernel(fmean_ref, fstd_ref, cost_ref, fmean_hbm, fstd_hbm, cost_hbm, sem):
+    copies = [
+        pltpu.make_async_copy(src, dst, sem.at[at])
+        for at, (src, dst) in enumerate(
+            ((fmean_ref, fmean_hbm), (fstd_ref, fstd_hbm), (cost_ref, cost_hbm))
+        )
+    ]
+    for copy in copies:
+        copy.start()
+    for copy in copies:
+        copy.wait()
 
 
 def shards(
@@ -445,11 +532,18 @@
             pltpu.VMEM((iters, 1, LANES), f32),
             pltpu.VMEM((iters, n_cand * n_env, 1, LANES), f32),
             pltpu.SemaphoreType.DMA((len(operands) + 1,)),
-            pltpu.SemaphoreType.DMA((iters, 3)),
-            pltpu.SemaphoreType.DMA((iters, 3)),
+            pltpu.SemaphoreType.DMA((iters, 5)),
+            pltpu.SemaphoreType.DMA((iters, 5)),
         ],
         compiler_params=pltpu.CompilerParams(collective_id=0, has_side_effects=True),
     )(*operands)
+    fmean, fstd, cost = pl.pallas_call(
+        store_kernel,
+        out_shape=tuple(jax.ShapeDtypeStruct(shape, kind) for shape, kind in outs),
+        in_specs=[vmem] * len(outs),
+        out_specs=(hbm, hbm, hbm),
+        scratch_shapes=[pltpu.SemaphoreType.DMA((len(outs),))],
+    )(*(pltpu.with_memory_space_constraint(x, pltpu.VMEM) for x in (fmean, fstd, cost)))
     return fmean, fstd, jnp.swapaxes(cost, 1, 2)
 
 

time: 50.6 us -> 44 us (0.87)
  Pallas kernels: 47.9 us -> 43 us
  local copies, waits for them, and re-layouts: 1.93 us -> 0 us
    pallas_call x1, Pallas kernels: 47.9 us -> 42.3 us  [shards(): pl.pallas_call(functools.partial(plan_kernel, dims), out_shape=tuple((plt...]
    unnamed x3 -> x0, local copies, waits for them, and re-layouts: 1.93 us -> none
    pallas_call x0 -> x1, Pallas kernels: none -> 0.75 us  [shards(): pl.pallas_call(store_kernel, out_shape=tuple((jax.ShapeDtypeStruct(shape,...]
where the time goes in v2:
time: 44 us; the launch traced here: 43.8 us
  Pallas kernels  43 us (98%)
  between operations  0.8 us (2%)
    pallas_call x1, Pallas kernels, shards(): pl.pallas_call(functools.partial(plan_kernel, dims), out_shape=tuple((plt...  42.3 us

profile of v2, /device:TPU:0, one launch (start us, length us, event | category | flops | bytes accessed | tf_op | source)
XLA Modules:
  0.0 43.8 jit_solution(16795472083925476086)
XLA Ops:
  0.6 42.3 %shard_map.139 = (f32[16,2560]{1,0:T(8,128)S(1)}, f32[16,2560]{1,0:T(8,128)S(1)}, f32[3,8,16]{2,1,0:T(8,128)S(1)}) custom-call(bf16[384,4096]{1,0:T(8,128)(2,1)} %bitcast.5, f32[16,2560]{1,0:T(8,128)} %mean_hbm.1, f32[16,2560]{1,0:T(8,128)} %std_hbm.1, f32[16,128]{1,0:T(8,128)} %start_hbm.1, f32[16,128]{1,0:T(8,128)} %goal_hbm.1, bf16[128,512]{1,0:T(8,128)(2,1)} %ws_hbm.1, ...), custom_call_target="tpu_custom_call" | custom-call | tf_op jit(solution)/shard_map/pallas_call | solution.py:512
  42.9 0.8 %shard_map.140 = (f32[16,2560]{1,0:T(8,128)}, f32[16,2560]{1,0:T(8,128)}, f32[3,8,16]{2,1,0:T(8,128)}) custom-call(f32[16,2560]{1,0:T(8,128)S(1)} %get-tuple-element.9.fmean_ref, f32[16,2560]{1,0:T(8,128)S(1)} %get-tuple-element.10.fstd_ref, f32[3,8,16]{2,1,0:T(8,128)S(1)} %get-tuple-element.11.cost_ref), custom_call_target="tpu_custom_call" | custom-call | tf_op jit(solution)/shard_map/pallas_call | solution.py:540

commit v3 on v2

--- a/solution.py
+++ b/solution.py
@@ -21,13 +21,13 @@
 WHILE_EARLY = (
     ((((0, 0),), 2, 1, (1, 0)),),
     ((((0, 6), (1, 0)), 2, 1, (2, 0)),),
-    ((((2, 0), (1, 6)), 2, 2, None),),
+    ((((2, 0), (1, 6)), 1, 2, None), (((2, 2), (1, 8)), 1, 2, None)),
 )
 WHILE_LATE = ((), (), ())
 WHILE_PEAKS = (
     ((((0, 2),), 3, 1, (1, 4)), (((0, 5),), 1, 1, None)),
     ((((0, 8), (1, 2)), 2, 1, (2, 4)), (((1, 4),), 1, 1, (2, 8)), (((1, 5),), 1, 1, None)),
-    ((((2, 4),), 3, 2, None),),
+    ((((2, 4),), 1, 2, None), (((2, 6),), 1, 2, None), (((2, 8),), 1, 2, None)),
 )
 
 
@@ -136,15 +136,16 @@
 
     def every_peer(visit):
         if n_all <= 64:
-            for k in range(1, n_all):
+            for k in range(n_all - 1, 0, -1):
                 visit(k)
         else:
             lax.fori_loop(1, n_all, lambda k, carry: (visit(k), carry)[1], 0)
 
     barrier = pltpu.get_barrier_semaphore()
-    every_peer(
-        lambda k: pl.semaphore_signal(barrier, inc=1, device_id=peer_of(k), device_id_type=MESH)
-    )
+    for axis, place, number in (("cand", me, n_cand), ("env", me_env, n_env)):
+        for o in range(1, number):
+            other = {axis: lax.rem(place + o, number)}
+            pl.semaphore_signal(barrier, inc=1, device_id=other, device_id_type=MESH)
 
     q = WIDE // act
     eye = (
@@ -274,25 +275,31 @@
 
         lax.fori_loop(first, first + count, one, 0)
 
-    parts = 2 if units == n_units and n_cand % 2 == 0 and out_blocks % 2 == 0 else 1
-    crowd = n_cand // parts
-    near = me // crowd
-
     lots = ((0, share // 2), (share // 2, share - share // 2)) if share > 1 else ((0, share),)
     sums_stage, means_stage, peaks_stage = 0, len(lots), 2 * len(lots)
 
-    def send_sums(it, part_at, far, lot):
+    def split(parts):
+        even = units == n_units and n_cand % parts == 0 and tiles % parts == 0
+        return parts if even else 1
+
+    def send_to(it, peer, slot, lot):
         low, size = lots[lot]
-        for o in range(0 if far else 1, crowd):
-            peer = part_at * crowd + lax.rem(lax.rem(me, crowd) + o, crowd)
-            pltpu.make_async_remote_copy(
-                src_ref=part.at[it, pl.ds(peer * share + low, size)],
-                dst_ref=rs_recv.at[it, o if far else n_cand - crowd + o - 1, pl.ds(low, size)],
-                send_sem=send_sem.at[it, sums_stage + lot],
-                recv_sem=recv_sem.at[it, sums_stage + lot],
-                device_id={"cand": peer},
-                device_id_type=MESH,
-            ).start()
+        pltpu.make_async_remote_copy(
+            src_ref=part.at[it, pl.ds(peer * share + low, size)],
+            dst_ref=rs_recv.at[it, slot, pl.ds(low, size)],
+            send_sem=send_sem.at[it, sums_stage + lot],
+            recv_sem=recv_sem.at[it, sums_stage + lot],
+            device_id={"cand": peer},
+            device_id_type=MESH,
+        ).start()
+
+    def send_sums(it, parts, k, lot):
+        crowd = n_cand // parts
+        near = int(k == parts - 1)
+        at = lax.rem(me // crowd + 1 + k, parts)
+        for o in range(near, crowd):
+            peer = at * crowd + lax.rem(lax.rem(me, crowd) + o, crowd)
+            send_to(it, peer, k * crowd + o - near, lot)
 
     def send_means(it, lot):
         low, size = lots[lot]
@@ -402,25 +409,53 @@
         for chains, count, span, paint in groups:
             rollout(chains, count, span, paint)
 
+    everything = range(len(lots))
+
+    def open_far(half):
+        crowd, some = n_cand // 2, tiles // 2
+        size = half + half % 2
+        early = size - 2
+        early_tiles = early * (WIDE // LANES)
+        served = early_tiles * halves // share
+        at = 1 - me // crowd
+        mine = lax.rem(me, crowd)
+        color(0, at * (out_blocks - early), early, early)
+        make_actions(0, None, at * (tiles - early_tiles), early_tiles)
+        pl.semaphore_wait(barrier, n_cand - 1 + n_env - 1)
+        for j in range(served):
+            rank = at * (crowd - served) + lax.rem(mine + j, served)
+            for lot in everything:
+                send_to(0, at * crowd + rank, lax.rem(rank - mine + crowd, crowd), lot)
+        color(0, early + at * (out_blocks - 2 * early - 2), 2, 2)
+        make_actions(0, None, early_tiles + at * (some - early_tiles), some - early_tiles)
+        for j in range(crowd - served):
+            rank = (1 - at) * served + j
+            for lot in everything:
+                send_to(0, at * crowd + rank, lax.rem(rank - mine + crowd, crowd), lot)
+
     loads[1].wait()
     scales = None
-    half = out_blocks // parts
-    everything = range(len(lots))
     for it in range(iters):
+        parts = split(4 if it else 2)
+        count = tiles // parts
         for k in range(parts):
-            far = k < parts - 1
-            at = lax.rem(near + 1 + k, parts)
+            at = lax.rem(me // (n_cand // parts) + 1 + k, parts)
             if it == 0:
-                color(0, at * half, half, half)
-            make_actions(it, scales, at * (tiles // parts), tiles // parts)
+                half = out_blocks // parts
+                if parts == 2 and k == 0 and half > 2:
+                    open_far(half)
+                    continue
+                size = half - half % 2 if parts == 2 and half > 2 else half
+                color(0, at * (out_blocks - size), size, size)
+            make_actions(it, scales, at * count, count)
             if it == 0 and k == 0:
-                pl.semaphore_wait(barrier, n_all - 1)
+                pl.semaphore_wait(barrier, n_cand - 1 + n_env - 1)
             for lot in everything if it == 0 or parts == 1 else (0,):
-                send_sums(it, at, far, lot)
+                send_sums(it, parts, k, lot)
         if it and parts > 1:
             for k in range(parts):
                 for lot in everything[1:]:
-                    send_sums(it, lax.rem(near + 1 + k, parts), k < parts - 1, lot)
+                    send_sums(it, parts, k, lot)
         if it == 0:
             set_rest()
         work(WHILE_EARLY[it])

time: 44 us -> 43.2 us (0.982)
  Pallas kernels: 43 us -> 42.2 us
    pallas_call x1, Pallas kernels: 42.3 us -> 41.4 us  [shards(): pl.pallas_call(functools.partial(plan_kernel, dims), out_shape=tuple((plt...]
where the time goes in v3:
time: 43.2 us; the launch traced here: 43 us
  Pallas kernels  42.2 us (98%)
  between operations  0.8 us (2%)
    pallas_call x1, Pallas kernels, shards(): pl.pallas_call(functools.partial(plan_kernel, dims), out_shape=tuple((plt...  41.4 us

profile of v3, /device:TPU:0, one launch (start us, length us, event | category | flops | bytes accessed | tf_op | source)
XLA Modules:
  0.0 43.0 jit_solution(5236244745391852953)
XLA Ops:
  0.6 41.4 %shard_map.139 = (f32[16,2560]{1,0:T(8,128)S(1)}, f32[16,2560]{1,0:T(8,128)S(1)}, f32[3,8,16]{2,1,0:T(8,128)S(1)}) custom-call(bf16[384,4096]{1,0:T(8,128)(2,1)} %bitcast.5, f32[16,2560]{1,0:T(8,128)} %mean_hbm.1, f32[16,2560]{1,0:T(8,128)} %std_hbm.1, f32[16,128]{1,0:T(8,128)} %start_hbm.1, f32[16,128]{1,0:T(8,128)} %goal_hbm.1, bf16[128,512]{1,0:T(8,128)(2,1)} %ws_hbm.1, ...), custom_call_target="tpu_custom_call" | custom-call | tf_op jit(solution)/shard_map/pallas_call | solution.py:547
  42.1 0.8 %shard_map.140 = (f32[16,2560]{1,0:T(8,128)}, f32[16,2560]{1,0:T(8,128)}, f32[3,8,16]{2,1,0:T(8,128)}) custom-call(f32[16,2560]{1,0:T(8,128)S(1)} %get-tuple-element.9.fmean_ref, f32[16,2560]{1,0:T(8,128)S(1)} %get-tuple-element.10.fstd_ref, f32[3,8,16]{2,1,0:T(8,128)S(1)} %get-tuple-element.11.cost_ref), custom_call_target="tpu_custom_call" | custom-call | tf_op jit(solution)/shard_map/pallas_call | solution.py:575

commit v4 on v3

--- a/solution.py
+++ b/solution.py
@@ -20,14 +20,18 @@
 TRIPS = 10
 WHILE_EARLY = (
     ((((0, 0),), 2, 1, (1, 0)),),
-    ((((0, 6), (1, 0)), 2, 1, (2, 0)),),
-    ((((2, 0), (1, 6)), 1, 2, None), (((2, 2), (1, 8)), 1, 2, None)),
+    ((((0, 5), (1, 0)), 2, 1, (2, 0)),),
+    ((((2, 0), (1, 5)), 1, 2, None), (((2, 2), (1, 7)), 1, 2, None)),
 )
-WHILE_LATE = ((), (), ())
+WHILE_LATE = (
+    (),
+    (),
+    (),
+)
 WHILE_PEAKS = (
-    ((((0, 2),), 3, 1, (1, 4)), (((0, 5),), 1, 1, None)),
-    ((((0, 8), (1, 2)), 2, 1, (2, 4)), (((1, 4),), 1, 1, (2, 8)), (((1, 5),), 1, 1, None)),
-    ((((2, 4),), 1, 2, None), (((2, 6),), 1, 2, None), (((2, 8),), 1, 2, None)),
+    ((((0, 2),), 3, 1, (1, 4)),),
+    ((((0, 7), (1, 2)), 3, 1, (2, 4)),),
+    ((((2, 4), (1, 9)), 1, 1, None), (((2, 5),), 1, 1, None), (((2, 6),), 1, 2, None), (((2, 8),), 1, 2, None)),
 )
 
 

time: 43.2 us -> 42.9 us (level)
  no operation moved by 1% of the time
where the time goes in v4:
time: 42.9 us; the launch traced here: 42.7 us
  Pallas kernels  41.9 us (98%)
  between operations  0.8 us (2%)
    pallas_call x1, Pallas kernels, shards(): pl.pallas_call(functools.partial(plan_kernel, dims), out_shape=tuple((plt...  41.1 us

profile of v4, /device:TPU:0, one launch (start us, length us, event | category | flops | bytes accessed | tf_op | source)
XLA Modules:
  0.0 42.7 jit_solution(7439057455805203178)
XLA Ops:
  0.6 41.1 %shard_map.139 = (f32[16,2560]{1,0:T(8,128)S(1)}, f32[16,2560]{1,0:T(8,128)S(1)}, f32[3,8,16]{2,1,0:T(8,128)S(1)}) custom-call(bf16[384,4096]{1,0:T(8,128)(2,1)} %bitcast.5, f32[16,2560]{1,0:T(8,128)} %mean_hbm.1, f32[16,2560]{1,0:T(8,128)} %std_hbm.1, f32[16,128]{1,0:T(8,128)} %start_hbm.1, f32[16,128]{1,0:T(8,128)} %goal_hbm.1, bf16[128,512]{1,0:T(8,128)(2,1)} %ws_hbm.1, ...), custom_call_target="tpu_custom_call" | custom-call | tf_op jit(solution)/shard_map/pallas_call | solution.py:551
  41.8 0.8 %shard_map.140 = (f32[16,2560]{1,0:T(8,128)}, f32[16,2560]{1,0:T(8,128)}, f32[3,8,16]{2,1,0:T(8,128)}) custom-call(f32[16,2560]{1,0:T(8,128)S(1)} %get-tuple-element.9.fmean_ref, f32[16,2560]{1,0:T(8,128)S(1)} %get-tuple-element.10.fstd_ref, f32[3,8,16]{2,1,0:T(8,128)S(1)} %get-tuple-element.11.cost_ref), custom_call_target="tpu_custom_call" | custom-call | tf_op jit(solution)/shard_map/pallas_call | solution.py:579
